TPU v7x, 32 devices: a whole 2x2x4 slice. The times are simulated.
32 devices in a mesh: group: 4 (over x, core), theta: 4 (over z), radial: 2 (over y).
Axes of the slice: x: 2, y: 2, z: 4, core: 2. Of those that a mesh axis runs over, the one named last changes fastest.
Arguments:
- scalars: float32 [26, 16, 16, 2048], P(None, 'group', 'radial', 'theta'), may hold values from 0.1 to 2
- axial_speed: float32 [16, 16, 2048], P('group', 'radial', 'theta'), may hold values from 0.2 to 0.9
- mixing: float32 [16, 16, 2048], P('group', 'radial', 'theta'), may hold values from 0.02 to 0.12
- reaction_rate: float32 [16, 16, 2048], P('group', 'radial', 'theta'), may hold values from 0.05 to 0.5
- reaction: float32 [20, 20], replicated, may hold values from -1.25 to 1.25
- nucleation: float32 [6], replicated, may hold values from 0.1 to 1
- coagulation: float32 [6], replicated, may hold values from 0.05 to 0.5
- inflow: float32 [26, 16, 2048], P(None, 'radial', 'theta'), may hold values from 0.1 to 2
- tile_weights: float32 [16, 128, 128], P('theta'), may hold values from -0.5 to 0.5
- donor_shift: int32 [16], P('theta'), may hold values from -1 to 1, as said below
- rotor_offset: int32 [1], replicated, may hold values from 0 to 2047
Outputs:
- advanced: float32 [26, 16, 16, 2048], P(None, 'group', 'radial', 'theta')
Inputs may be any that keep to these rules, and one draw needn't show every extreme that they name: `donor_shift`: in every aligned block of 4 tiles the first tile has offset -1 and the last offset 1.
All inputs are finite; a program needn't handle non-finite values.
Results may differ from a plain program's by a relative error of at most 0.00005.
Values sent between devices are 32-bit elements; how exact they have to be, the bound alone decides.
No kernel may reach another device: no remote copies, remote signals or barrier semaphores. Data moves between devices by JAX's collectives and lax.ppermute only.
A program may use at most 64 MiB of HBM per device.

v0:
```python
import jax
import jax.numpy as jnp
from jax import lax
from jax.sharding import PartitionSpec as P

SPECIES = 20
highest = lax.Precision.HIGHEST


def from_behind(block, axis, distance):
    devices = range(lax.axis_size(axis))
    route = [((i - distance) % len(devices), i) for i in devices]
    return lax.ppermute(block, axis, route)


def padded(array, sides, width, wrap):
    for axis, dim in sides:
        count, length = (lax.axis_size(axis), array.shape[dim])
        up = [(i, (i + 1) % count) for i in range(count if wrap else count - 1)]
        down = [(j, i) for i, j in up]
        last = lax.slice_in_dim(array, length - width, length, axis=dim)
        initial = lax.slice_in_dim(array, 0, width, axis=dim)
        before = lax.ppermute(last, axis, up)
        after = lax.ppermute(initial, axis, down)
        array = jnp.concatenate([before, array, after], axis=dim)
    return array


def from_behind_2(array, axis, by):
    count = lax.axis_size(axis)
    pairs = [(i, i + by) for i in range(count) if 0 <= i + by < count]
    return lax.ppermute(array, axis, pairs)


def rotate_rows(plane_rows, rotor_offset):
    sectors = lax.axis_size("theta")
    theta_cells = plane_rows.shape[1]
    device_hops = rotor_offset[0] // theta_cells
    cell_shift = rotor_offset[0] % theta_cells
    scattered = lax.all_to_all(plane_rows[None], "theta", split_axis=2, concat_axis=0, tiled=True)
    doubled = jnp.concatenate([scattered, scattered], axis=0)
    turned = lax.dynamic_slice_in_dim(doubled, sectors - device_hops, sectors, 0)
    shifted = lax.all_to_all(turned, "theta", split_axis=0, concat_axis=2, tiled=True)[0]
    previous = from_behind(shifted, "theta", 1)
    joined = jnp.concatenate([previous, shifted], axis=1)
    return lax.dynamic_slice_in_dim(joined, theta_cells - cell_shift, theta_cells, 1)


def apply_tiles(picked_rows, tile_weights):
    row_count, theta_cells = picked_rows.shape
    tile_blocks = picked_rows.reshape(row_count, theta_cells // 128, 128)
    result = jnp.einsum("rtk,tjk->rtj", tile_blocks, tile_weights, precision=highest)
    return result.reshape(row_count, theta_cells)


def couple_cells(plane_rows, tile_weights, donor_shift, rotor_offset):
    row_count, theta_cells = plane_rows.shape
    tile_count = theta_cells // 128
    rotated = rotate_rows(plane_rows, rotor_offset)
    extended = padded(rotated, (("theta", 1),), 128, True)
    tile_blocks = extended.reshape(row_count, tile_count + 2, 128)
    columns = lax.broadcasted_iota(jnp.int32, (tile_count, tile_count + 2), 1)
    targets = (
        lax.broadcasted_iota(jnp.int32, (tile_count, tile_count + 2), 0) + 1 + donor_shift[:, None]
    )
    chooser = (columns == targets).astype(jnp.float32)
    picked = jnp.einsum("rsk,ts->rtk", tile_blocks, chooser, precision=highest)
    return apply_tiles(picked.reshape(row_count, theta_cells), tile_weights)


def couple_rows(plane_rows, tile_weights, donor_shift, rotor_offset):
    return couple_cells(plane_rows, tile_weights, donor_shift, rotor_offset)


def local(
    scalars,
    axial_speed,
    mixing,
    reaction_rate,
    reaction,
    nucleation,
    coagulation,
    inflow,
    tile_weights,
    donor_shift,
    rotor_offset,
):
    variables, layers, radial_cells, theta_cells = scalars.shape
    groups = lax.axis_size("group")
    group_index = lax.axis_index("group")
    row_count = variables * radial_cells
    last_layer = scalars[:, layers - 1]
    received = from_behind_2(last_layer, "group", 1)
    coupled = couple_rows(
        received.reshape(row_count, theta_cells), tile_weights, donor_shift, rotor_offset
    )
    coupled = coupled.reshape(variables, radial_cells, theta_cells)
    ghost_plane = jnp.where(
        group_index == 0, inflow, jnp.where(group_index == groups - 1, coupled, received)
    )
    upstream = jnp.concatenate([ghost_plane[:, None], scalars[:, :-1]], axis=1)
    circle = padded(scalars, (("theta", 3),), 1, True)
    walls = padded(scalars, (("radial", 2),), 1, False)
    beside_all = circle[:, :, :, :-2] + circle[:, :, :, 2:]
    beside_all = beside_all + walls[:, :, 2:] + walls[:, :, :-2]
    laplace_term = beside_all - 4.0 * scalars
    species = scalars[:SPECIES]
    moments = scalars[SPECIES:]
    produced = jnp.dot(
        reaction,
        species.reshape(SPECIES, -1),
        precision=highest,
        preferred_element_type=jnp.float32,
    ).reshape(species.shape)
    growth = (
        nucleation[:, None, None, None] * species[SPECIES - 1]
        - coagulation[:, None, None, None] * moments[0] * moments
    )
    sources = jnp.concatenate([produced, growth], axis=0) * reaction_rate
    return scalars - axial_speed * (scalars - upstream) + mixing * laplace_term + sources


def solution(mesh):
    placed = (
        P(None, "group", "radial", "theta"),
        P("group", "radial", "theta"),
        P("group", "radial", "theta"),
        P("group", "radial", "theta"),
        P(),
        P(),
        P(),
        P(None, "radial", "theta"),
        P("theta", None, None),
        P("theta"),
        P(),
    )
    return jax.shard_map(
        local,
        mesh=mesh,
        in_specs=placed,
        out_specs=P(None, "group", "radial", "theta"),
        check_vma=False,
    )
```

profile of v0, /device:TPU:2, one launch (start us, length us, event | category | flops | bytes accessed | tf_op | source)
XLA Modules:
  0.0 98.0 jit_solution(16897832875728588099)
XLA Ops:
  0.0 2.5 %copy.82 = f32[26,4,8,512]{3,0,2,1:T(8,128)S(1)} copy(f32[26,4,8,512]{3,2,1,0:T(8,128)} %param.11) | data formatting | bytes 3407872 | tf_op args[0]
  2.6 1.9 %collective-permute-start = (f32[26,8,512]{2,0,1:T(8,128)S(1)}, f32[26,8,512]{2,0,1:T(8,128)S(1)}, u32[]{:S(2)}, u32[]{:S(2)}) collective-permute-start(f32[26,8,512]{2,0,1:T(8,128)S(1)} %slice_bitcast_fusion.2), channel_id=1, source_target_pairs={{0,8},{8,16},{16,24},{1,9},{9,17},{17,25},{2,10},{10,18},{18,26},{... | collective-permute-start | bytes 1277960 | tf_op jit(solution)/shard_map/ppermute | solution.py:32
  4.5 8.6 %collective-permute-done = f32[26,8,512]{2,0,1:T(8,128)S(1)} collective-permute-done((f32[26,8,512]{2,0,1:T(8,128)S(1)}, f32[26,8,512]{2,0,1:T(8,128)S(1)}, u32[]{:S(2)}, u32[]{:S(2)}) %collective-permute-start) | collective-permute-done | bytes 426016 | tf_op jit(solution)/shard_map/ppermute | solution.py:32
  13.1 0.8 copy-done.4
  14.1 1.0 %copy.73 = f32[1,208,512]{1,0,2:T(1,128)} copy(f32[1,208,512]{2,1,0:T(8,128)S(1)} %bitcast.63) | data formatting | bytes 851968 | tf_op jit(solution)/shard_map/broadcast_in_dim;reshape | solution.py:40
  15.1 4.9 %all-to-all-start = ((f32[1,208,512]{1,0,2:T(1,128)}), f32[1,208,512]{1,0,2:T(1,128)S(1)}, u32[]{:S(2)}, u32[]{:S(2)}) async-start(f32[1,208,512]{1,0,2:T(1,128)} %copy.73), calls=%async_computation | async-start | bytes 1048576 | tf_op jit(solution)/shard_map/all_to_all | solution.py:40
  20.0 0.8 fusion.21
  20.8 1.3 %collective-permute-start.6 = (f32[26,4,1,512]{3,0,2,1:T(8,128)}, f32[26,4,1,512]{3,0,2,1:T(8,128)}, u32[]{:S(2)}, u32[]{:S(2)}) collective-permute-start(f32[26,4,1,512]{3,0,2,1:T(8,128)} %get-tuple-element.7), channel_id=1, source_target_pairs={{1,0},{3,2},{5,4},{7,6},{9,8},{11,10},{13,12},{15,14},{17,16},{19,... | collective-permute-start | bytes 638984 | tf_op jit(solution)/shard_map/ppermute | solution.py:24
  22.2 6.1 %collective-permute-start.7 = (f32[26,4,1,512]{3,0,2,1:T(8,128)}, f32[26,4,1,512]{3,0,2,1:T(8,128)}, u32[]{:S(2)}, u32[]{:S(2)}) collective-permute-start(f32[26,4,1,512]{3,0,2,1:T(8,128)} %get-tuple-element.8), channel_id=1, source_target_pairs={{0,1},{2,3},{4,5},{6,7},{8,9},{10,11},{12,13},{14,15},{16,17},{18,... | collective-permute-start | bytes 638984 | tf_op jit(solution)/shard_map/ppermute | solution.py:23
  28.2 1.1 %fusion.20 = (f32[26,4,8,1]{3,0,2,1:T(8,128)}, f32[26,4,8,1]{3,0,2,1:T(8,128)}) fusion(f32[26,4,8,512]{3,0,2,1:T(8,128)S(1)} %copy.82), kind=kLoop, calls=%fused_computation.44 | loop fusion | bytes 13312 | tf_op jit(solution)/shard_map/slice | solution.py:21
  29.4 2.0 %collective-permute-start.4 = (f32[26,4,8,1]{3,0,2,1:T(8,128)}, f32[26,4,8,1]{3,0,2,1:T(8,128)}, u32[]{:S(2)}, u32[]{:S(2)}) collective-permute-start(f32[26,4,8,1]{3,0,2,1:T(8,128)} %get-tuple-element.5), channel_id=1, source_target_pairs={{0,2},{2,4},{4,6},{6,0},{1,3},{3,5},{5,7},{7,1},{8,10},{10,12},{12... | collective-permute-start | bytes 9992 | tf_op jit(solution)/shard_map/ppermute | solution.py:23
  32.1 8.1 %all-to-all-done = f32[1,208,512]{1,0,2:T(1,128)S(1)} async-done(((f32[1,208,512]{1,0,2:T(1,128)}), f32[1,208,512]{1,0,2:T(1,128)S(1)}, u32[]{:S(2)}, u32[]{:S(2)}) %all-to-all-start) | async-done | bytes 426016 | tf_op jit(solution)/shard_map/all_to_all | solution.py:40
  40.1 0.3 copy.74
  40.5 0.8 fusion.14
  41.3 3.5 %all-to-all-start.1 = ((f32[4,208,128]{2,1,0:T(8,128)}), f32[4,208,128]{2,1,0:T(8,128)S(1)}, u32[]{:S(2)}, u32[]{:S(2)}) async-start(f32[4,208,128]{2,1,0:T(8,128)} %fusion.14), calls=%async_computation.1 | async-start | bytes 851968 | tf_op jit(solution)/shard_map/all_to_all | solution.py:43
  44.8 0.9 slice_bitcast_fusion.4
  45.7 1.0 %fusion.11 = f32[6,4,8,512]{3,0,2,1:T(8,128)} fusion(f32[26,4,8,512]{3,0,2,1:T(8,128)S(1)} %copy.82, f32[4,8,512]{2,1,0:T(8,128)S(1)} %get-tuple-element.10, f32[6]{0:T(128)S(1)} %copy-done.9, f32[4,8,512]{2,1,0:T(8,128)S(1)} %get-tuple-element.9, f32[6]{0:T(128)S(1)} %copy-done.10), kind=kLoop, calls=%fused_computation.27 | loop fusion | flops 393216 | bytes 917552 | tf_op jit(solution)/shard_map/sub | solution.py:116
  46.7 2.5 %slice_bitcast_fusion.1 = f32[20,32,512]{2,1,0:T(8,128)} fusion(f32[26,4,8,512]{3,2,1,0:T(8,128)} %param.11), kind=kLoop, calls=%fused_computation.18 | loop fusion | bytes 2621440
  49.2 9.3 %all-to-all-done.1 = f32[4,208,128]{2,1,0:T(8,128)S(1)} async-done(((f32[4,208,128]{2,1,0:T(8,128)}), f32[4,208,128]{2,1,0:T(8,128)S(1)}, u32[]{:S(2)}, u32[]{:S(2)}) %all-to-all-start.1) | async-done | bytes 426016 | tf_op jit(solution)/shard_map/all_to_all | solution.py:43
  58.8 1.0 %copy-done.3 = f32[20,32,512]{2,1,0:T(8,128)S(1)} copy-done((f32[20,32,512]{2,1,0:T(8,128)S(1)}, f32[20,32,512]{2,1,0:T(8,128)}, u32[]{:S(2)}) %copy-start.3) | copy-done | bytes 1310744
  60.0 3.2 %fusion.9 = f32[20,4,8,512]{3,0,2,1:T(8,128)} fusion(f32[4,8,512,20]{2,1,0,3:T(8,128)S(1)} %slice_bitcast_fusion, f32[20,20]{1,0:T(8,128)S(1)} %copy-done.8), kind=kOutput, calls=%fused_computation.15 | convolution fusion | flops 78643200 | bytes 2623040 | tf_op jit(solution)/shard_map/dot_general | solution.py:109
  63.2 10.1 %collective-permute-done.1 = f32[208,512]{1,0:T(8,128)S(1)} collective-permute-done((f32[208,512]{1,0:T(8,128)S(1)}, f32[208,512]{1,0:T(8,128)S(1)}, u32[]{:S(2)}, u32[]{:S(2)}) %collective-permute-start.1) | collective-permute-done | bytes 426016 | tf_op jit(solution)/shard_map/ppermute | solution.py:13
  73.7 3.8 %collective-permute-start.3 = (f32[208,128]{1,0:T(8,128)S(1)}, f32[208,128]{1,0:T(8,128)S(1)}, u32[]{:S(2)}, u32[]{:S(2)}) collective-permute-start(f32[208,128]{1,0:T(8,128)S(1)} %get-tuple-element.12), channel_id=1, source_target_pairs={{2,0},{4,2},{6,4},{0,6},{3,1},{5,3},{7,5},{1,7},{10,8},{12,10},{14... | collective-permute-start | bytes 319496 | tf_op jit(solution)/shard_map/ppermute | solution.py:24
  77.5 2.7 %collective-permute-done.2 = f32[208,128]{1,0:T(8,128)S(1)} collective-permute-done((f32[208,128]{1,0:T(8,128)S(1)}, f32[208,128]{1,0:T(8,128)S(1)}, u32[]{:S(2)}, u32[]{:S(2)}) %collective-permute-start.2) | collective-permute-done | bytes 106528 | tf_op jit(solution)/shard_map/ppermute | solution.py:23
  80.3 0.6 convolution_bitcast_fusion.1
  80.9 0.6 convolution_bitcast_fusion
  81.5 0.9 copy.77
  82.5 1.9 %reshape_reshape.3 = f32[26,8,512]{2,1,0:T(8,128)} reshape(f32[208,4,128]{2,1,0:T(4,128)} %copy.77) | data formatting | bytes 851968 | tf_op jit(solution)/shard_map/reshape;reshape | solution.py:97
  84.4 1.9 %fusion.12 = f32[26,1,8,512]{3,0,2,1:T(8,128)S(1)} fusion(f32[26,8,512]{2,1,0:T(8,128)} %param.18, f32[26,8,512]{2,0,1:T(8,128)} %copy-done.4, f32[26,8,512]{2,1,0:T(8,128)} %reshape_reshape.3, pred[]{:T(512)S(6)} %eq.12, pred[]{:T(512)S(6)} %eq.11), kind=kLoop, calls=%fused_computation.30 | loop fusion | flops 212992 | bytes 1703938 | tf_op jit(solution)/shard_map/broadcast_in_dim | solution.py:101
  86.3 3.4 %collective-permute-done.5 = f32[26,4,8,1]{3,0,2,1:T(8,128)} collective-permute-done((f32[26,4,8,1]{3,0,2,1:T(8,128)}, f32[26,4,8,1]{3,0,2,1:T(8,128)}, u32[]{:S(2)}, u32[]{:S(2)}) %collective-permute-start.5) | collective-permute-done | bytes 3360 | tf_op jit(solution)/shard_map/ppermute | solution.py:24
  89.7 6.1 %fusion.4 = f32[26,4,8,512]{3,0,2,1:T(8,128)S(1)} fusion(f32[26,4,8,512]{3,0,2,1:T(8,128)} %copy-done.1, f32[26,4,1,512]{3,0,2,1:T(8,128)} %collective-permute-done.7, f32[26,4,1,512]{3,0,2,1:T(8,128)} %collective-permute-done.6, f32[26,4,8,1]{3,0,2,1:T(8,128)} %collective-permute-done.5, f32[26,4,8,1]{3,0,2,1:T(8,128)} %collective-permute-done.4, ...), kind=kLoop, calls=%fused_computation.5 | loop fusion | flops 7667712 | bytes 7444992 | tf_op jit(solution)/shard_map/add | solution.py:120
  95.8 2.2 %copy.94 = f32[26,4,8,512]{3,2,1,0:T(8,128)} copy(f32[26,4,8,512]{3,0,2,1:T(8,128)S(1)} %fusion.4) | data formatting | bytes 3407872 | tf_op jit(solution)/shard_map/add | solution.py:120
  (41 shorter events, 1.3 us)
Async XLA Ops:
  0.0 80.9 %copy-start = (f32[4,128,128]{2,1,0:T(8,128)S(1)}, f32[4,128,128]{2,1,0:T(8,128)}, u32[]{:S(2)}) copy-start(f32[4,128,128]{2,1,0:T(8,128)} %param.19) | copy-start | bytes 786436
  2.5 75.0 %copy-start.1 = (f32[26,4,8,512]{3,0,2,1:T(8,128)}, f32[26,4,8,512]{3,0,2,1:T(8,128)S(1)}, u32[]{:S(2)}) copy-start(f32[26,4,8,512]{3,0,2,1:T(8,128)S(1)} %copy.82) | copy-start | bytes 5111812
  2.6 10.5 %collective-permute-start = (f32[26,8,512]{2,0,1:T(8,128)S(1)}, f32[26,8,512]{2,0,1:T(8,128)S(1)}, u32[]{:S(2)}, u32[]{:S(2)}) collective-permute-start(f32[26,8,512]{2,0,1:T(8,128)S(1)} %slice_bitcast_fusion.2), channel_id=1, source_target_pairs={{0,8},{8,16},{16,24},{1,9},{9,17},{17,25},{2,10},{10,18},{18,26},{... | collective-permute-start | bytes 1277960 | tf_op jit(solution)/shard_map/ppermute | solution.py:32
  13.1 0.8 copy-start.4
  15.1 25.0 %all-to-all-start = ((f32[1,208,512]{1,0,2:T(1,128)}), f32[1,208,512]{1,0,2:T(1,128)S(1)}, u32[]{:S(2)}, u32[]{:S(2)}) async-start(f32[1,208,512]{1,0,2:T(1,128)} %copy.73), calls=%async_computation | async-start | bytes 1048576 | tf_op jit(solution)/shard_map/all_to_all | solution.py:40
  20.8 68.8 %collective-permute-start.6 = (f32[26,4,1,512]{3,0,2,1:T(8,128)}, f32[26,4,1,512]{3,0,2,1:T(8,128)}, u32[]{:S(2)}, u32[]{:S(2)}) collective-permute-start(f32[26,4,1,512]{3,0,2,1:T(8,128)} %get-tuple-element.7), channel_id=1, source_target_pairs={{1,0},{3,2},{5,4},{7,6},{9,8},{11,10},{13,12},{15,14},{17,16},{19,... | collective-permute-start | bytes 638984 | tf_op jit(solution)/shard_map/ppermute | solution.py:24
  22.1 23.5 %copy-start.9 = (f32[6]{0:T(128)S(1)}, f32[6]{0:T(128)}, u32[]{:S(2)}) copy-start(f32[6]{0:T(128)} %param.17) | copy-start | bytes 76
  22.1 23.5 %copy-start.10 = (f32[6]{0:T(128)S(1)}, f32[6]{0:T(128)}, u32[]{:S(2)}) copy-start(f32[6]{0:T(128)} %param.16) | copy-start | bytes 76
  22.2 67.5 %collective-permute-start.7 = (f32[26,4,1,512]{3,0,2,1:T(8,128)}, f32[26,4,1,512]{3,0,2,1:T(8,128)}, u32[]{:S(2)}, u32[]{:S(2)}) collective-permute-start(f32[26,4,1,512]{3,0,2,1:T(8,128)} %get-tuple-element.8), channel_id=1, source_target_pairs={{0,1},{2,3},{4,5},{6,7},{8,9},{10,11},{12,13},{14,15},{16,17},{18,... | collective-permute-start | bytes 638984 | tf_op jit(solution)/shard_map/ppermute | solution.py:23
  29.4 56.9 %collective-permute-start.4 = (f32[26,4,8,1]{3,0,2,1:T(8,128)}, f32[26,4,8,1]{3,0,2,1:T(8,128)}, u32[]{:S(2)}, u32[]{:S(2)}) collective-permute-start(f32[26,4,8,1]{3,0,2,1:T(8,128)} %get-tuple-element.5), channel_id=1, source_target_pairs={{0,2},{2,4},{4,6},{6,0},{1,3},{3,5},{5,7},{7,1},{8,10},{10,12},{12... | collective-permute-start | bytes 9992 | tf_op jit(solution)/shard_map/ppermute | solution.py:23
  41.3 17.2 %all-to-all-start.1 = ((f32[4,208,128]{2,1,0:T(8,128)}), f32[4,208,128]{2,1,0:T(8,128)S(1)}, u32[]{:S(2)}, u32[]{:S(2)}) async-start(f32[4,208,128]{2,1,0:T(8,128)} %fusion.14), calls=%async_computation.1 | async-start | bytes 851968 | tf_op jit(solution)/shard_map/all_to_all | solution.py:43
  58.5 1.3 %copy-start.3 = (f32[20,32,512]{2,1,0:T(8,128)S(1)}, f32[20,32,512]{2,1,0:T(8,128)}, u32[]{:S(2)}) copy-start(f32[20,32,512]{2,1,0:T(8,128)} %slice_bitcast_fusion.1) | copy-start | bytes 3932164
  58.5 1.5 %copy-start.8 = (f32[20,20]{1,0:T(8,128)S(1)}, f32[20,20]{1,0:T(8,128)}, u32[]{:S(2)}) copy-start(f32[20,20]{1,0:T(8,128)} %param.15) | copy-start | bytes 4804
  58.7 14.5 %collective-permute-start.1 = (f32[208,512]{1,0:T(8,128)S(1)}, f32[208,512]{1,0:T(8,128)S(1)}, u32[]{:S(2)}, u32[]{:S(2)}) collective-permute-start(f32[208,512]{1,0:T(8,128)S(1)} %bitcast.60), channel_id=1, source_target_pairs={{6,0},{0,2},{2,4},{4,6},{7,1},{1,3},{3,5},{5,7},{14,8},{8,10},{10,... | collective-permute-start | bytes 1277960 | tf_op jit(solution)/shard_map/ppermute | solution.py:13
  60.0 17.5 %copy-start.11 = (s32[4]{0:T(128)S(1)}, s32[4]{0:T(128)}, u32[]{:S(2)}) copy-start(s32[4]{0:T(128)} %param.20) | copy-start | bytes 52
  73.6 6.6 %collective-permute-start.2 = (f32[208,128]{1,0:T(8,128)S(1)}, f32[208,128]{1,0:T(8,128)S(1)}, u32[]{:S(2)}, u32[]{:S(2)}) collective-permute-start(f32[208,128]{1,0:T(8,128)S(1)} %get-tuple-element.11), channel_id=1, source_target_pairs={{0,2},{2,4},{4,6},{6,0},{1,3},{3,5},{5,7},{7,1},{8,10},{10,12},{12... | collective-permute-start | bytes 319496 | tf_op jit(solution)/shard_map/ppermute | solution.py:23
  73.7 6.5 %collective-permute-start.3 = (f32[208,128]{1,0:T(8,128)S(1)}, f32[208,128]{1,0:T(8,128)S(1)}, u32[]{:S(2)}, u32[]{:S(2)}) collective-permute-start(f32[208,128]{1,0:T(8,128)S(1)} %get-tuple-element.12), channel_id=1, source_target_pairs={{2,0},{4,2},{6,4},{0,6},{3,1},{5,3},{7,5},{1,7},{10,8},{12,10},{14... | collective-permute-start | bytes 319496 | tf_op jit(solution)/shard_map/ppermute | solution.py:24
  80.2 9.5 %collective-permute-start.5 = (f32[26,4,8,1]{3,0,2,1:T(8,128)}, f32[26,4,8,1]{3,0,2,1:T(8,128)}, u32[]{:S(2)}, u32[]{:S(2)}) collective-permute-start(f32[26,4,8,1]{3,0,2,1:T(8,128)} %get-tuple-element.6), channel_id=1, source_target_pairs={{2,0},{4,2},{6,4},{0,6},{3,1},{5,3},{7,5},{1,7},{10,8},{12,10},{14... | collective-permute-start | bytes 9992 | tf_op jit(solution)/shard_map/ppermute | solution.py:24
  80.9 8.8 %slice-start = ((f32[26,4,8,512]{3,0,2,1:T(8,128)}), f32[26,3,8,512]{3,0,2,1:T(8,128)S(1)}, s32[]{:S(2)}) async-start(f32[26,4,8,512]{3,0,2,1:T(8,128)} %copy-done.1), calls=%async_computation.2 | async-start | bytes 3145728 | tf_op jit(solution)/shard_map/slice | solution.py:101
  80.9 8.8 %copy-start.2 = (f32[20,4,8,512]{3,0,2,1:T(8,128)S(1)}, f32[20,4,8,512]{3,0,2,1:T(8,128)}, u32[]{:S(2)}) copy-start(f32[20,4,8,512]{3,0,2,1:T(8,128)} %fusion.9) | copy-start | bytes 3932164
  80.9 8.8 %copy-start.6 = (f32[4,8,512]{2,1,0:T(8,128)S(1)}, f32[4,8,512]{2,1,0:T(8,128)}, u32[]{:S(2)}) copy-start(f32[4,8,512]{2,1,0:T(8,128)} %param.14) | copy-start | bytes 196612
  80.9 8.8 %copy-start.7 = (f32[4,8,512]{2,1,0:T(8,128)S(1)}, f32[4,8,512]{2,1,0:T(8,128)}, u32[]{:S(2)}) copy-start(f32[4,8,512]{2,1,0:T(8,128)} %param.13) | copy-start | bytes 196612
  84.4 5.3 %copy-start.5 = (f32[6,4,8,512]{3,0,2,1:T(8,128)S(1)}, f32[6,4,8,512]{3,0,2,1:T(8,128)}, u32[]{:S(2)}) copy-start(f32[6,4,8,512]{3,0,2,1:T(8,128)} %fusion.11) | copy-start | bytes 1179652
where the time goes:
time: 98.5 us; the launch traced here: 98 us
  waiting for transfers between devices  42.1 us (43%)
  starting transfers between devices  23.6 us (24%)
  local copies, waits for them, and re-layouts  16.9 us (17%)
  other arithmetic  10.1 us (10%)
  matrix products  4.31 us (4%)
  between operations  0.99 us (1%)
    ppermute x1, waiting for transfers between devices, from_behind(): return lax.ppermute(block, axis, route)  10.1 us
    all_to_all x1, waiting for transfers between devices, rotate_rows(): lax.all_to_all(turned, 'theta', split_axis=0, concat_axis=2, tiled=True)[0]  9.34 us
    ppermute x1, waiting for transfers between devices, from_behind_2(): return lax.ppermute(array, axis, pairs)  8.57 us
    ppermute x3, starting transfers between devices, padded(): before = lax.ppermute(last, axis, up)  8.16 us
    all_to_all x1, waiting for transfers between devices, rotate_rows(): lax.all_to_all(plane_rows[None], 'theta', split_axis=2, concat_axis=0, ti...  8.06 us
    unnamed x27, local copies, waits for them, and re-layouts  6.92 us
    add x1, other arithmetic, local(): scalars - axial_speed * (scalars - upstream) + mixing * laplace_term  6.1 us
    ppermute x3, starting transfers between devices, padded(): after = lax.ppermute(initial, axis, down)  5.09 us
  transfers between devices with their start and end apart: 10, of which 6 were waited for; matrix products, arithmetic and copies ran while one was open for 18% of the time, Pallas kernels for 0%

commit v1 on v0

--- a/solution.py
+++ b/solution.py
@@ -5,6 +5,14 @@
 
 SPECIES = 20
 highest = lax.Precision.HIGHEST
+
+
+def replace_the_sections(base_x):
+    even = lax.axis_size("theta")
+    raw_out = jnp.split(base_x, even, axis=0)
+    outcome_arr = jnp.stack(raw_out)
+    current_value = lax.all_to_all(outcome_arr, "theta", 0, 0)
+    return jnp.concatenate(current_value, axis=2)
 
 
 def from_behind(block, axis, distance):
@@ -40,7 +48,7 @@
     scattered = lax.all_to_all(plane_rows[None], "theta", split_axis=2, concat_axis=0, tiled=True)
     doubled = jnp.concatenate([scattered, scattered], axis=0)
     turned = lax.dynamic_slice_in_dim(doubled, sectors - device_hops, sectors, 0)
-    shifted = lax.all_to_all(turned, "theta", split_axis=0, concat_axis=2, tiled=True)[0]
+    shifted = replace_the_sections(turned)[0]
     previous = from_behind(shifted, "theta", 1)
     joined = jnp.concatenate([previous, shifted], axis=1)
     return lax.dynamic_slice_in_dim(joined, theta_cells - cell_shift, theta_cells, 1)

time: 98.5 us -> 98.8 us (level)
  no operation moved by 1% of the time
where the time goes in v1:
time: 98.8 us; the launch traced here: 98.3 us
  waiting for transfers between devices  42.3 us (43%)
  starting transfers between devices  23.5 us (24%)
  local copies, waits for them, and re-layouts  17 us (17%)
  other arithmetic  10.3 us (10%)
  matrix products  4.31 us (4%)
  between operations  0.99 us (1%)
    ppermute x1, waiting for transfers between devices, from_behind(): return lax.ppermute(block, axis, route)  10.1 us
    all_to_all x1, waiting for transfers between devices, replace_the_sections(): current_value = lax.all_to_all(outcome_arr, 'theta', 0, 0)  9.32 us
    ppermute x1, waiting for transfers between devices, from_behind_2(): return lax.ppermute(array, axis, pairs)  8.57 us
    all_to_all x1, waiting for transfers between devices, rotate_rows(): lax.all_to_all(plane_rows[None], 'theta', split_axis=2, concat_axis=0, ti...  8.27 us
    ppermute x3, starting transfers between devices, padded(): before = lax.ppermute(last, axis, up)  8.05 us
    unnamed x27, local copies, waits for them, and re-layouts  6.91 us
    add x1, other arithmetic, local(): scalars - axial_speed * (scalars - upstream) + mixing * laplace_term  6.18 us
    ppermute x3, starting transfers between devices, padded(): after = lax.ppermute(initial, axis, down)  5.09 us
  transfers between devices with their start and end apart: 10, of which 6 were waited for; matrix products, arithmetic and copies ran while one was open for 18% of the time, Pallas kernels for 0%

profile of v1, /device:TPU:2, one launch (start us, length us, event | category | flops | bytes accessed | tf_op | source)
XLA Modules:
  0.0 98.3 jit_solution(1481095927739889467)
XLA Ops:
  0.0 2.5 %copy.66 = f32[26,4,8,512]{3,0,2,1:T(8,128)S(1)} copy(f32[26,4,8,512]{3,2,1,0:T(8,128)} %param.11) | data formatting | bytes 3407872 | tf_op args[0]
  2.6 1.9 %collective-permute-start = (f32[26,8,512]{2,0,1:T(8,128)S(1)}, f32[26,8,512]{2,0,1:T(8,128)S(1)}, u32[]{:S(2)}, u32[]{:S(2)}) collective-permute-start(f32[26,8,512]{2,0,1:T(8,128)S(1)} %slice_bitcast_fusion.2), channel_id=1, source_target_pairs={{0,8},{8,16},{16,24},{1,9},{9,17},{17,25},{2,10},{10,18},{18,26},{... | collective-permute-start | bytes 1277960 | tf_op jit(solution)/shard_map/ppermute | solution.py:40
  4.5 8.6 %collective-permute-done = f32[26,8,512]{2,0,1:T(8,128)S(1)} collective-permute-done((f32[26,8,512]{2,0,1:T(8,128)S(1)}, f32[26,8,512]{2,0,1:T(8,128)S(1)}, u32[]{:S(2)}, u32[]{:S(2)}) %collective-permute-start) | collective-permute-done | bytes 426016 | tf_op jit(solution)/shard_map/ppermute | solution.py:40
  13.1 0.8 copy-done.4
  14.1 1.0 %copy.57 = f32[1,208,512]{1,0,2:T(1,128)} copy(f32[1,208,512]{2,1,0:T(8,128)S(1)} %bitcast.69) | data formatting | bytes 851968 | tf_op jit(solution)/shard_map/broadcast_in_dim;reshape | solution.py:48
  15.1 4.9 %all-to-all-start = ((f32[1,208,512]{1,0,2:T(1,128)}), f32[1,208,512]{1,0,2:T(1,128)S(1)}, u32[]{:S(2)}, u32[]{:S(2)}) async-start(f32[1,208,512]{1,0,2:T(1,128)} %copy.57), calls=%async_computation | async-start | bytes 1048576 | tf_op jit(solution)/shard_map/all_to_all | solution.py:48
  20.0 0.8 fusion.21
  20.9 1.3 %collective-permute-start.6 = (f32[26,4,1,512]{3,0,2,1:T(8,128)}, f32[26,4,1,512]{3,0,2,1:T(8,128)}, u32[]{:S(2)}, u32[]{:S(2)}) collective-permute-start(f32[26,4,1,512]{3,0,2,1:T(8,128)} %get-tuple-element.7), channel_id=1, source_target_pairs={{1,0},{3,2},{5,4},{7,6},{9,8},{11,10},{13,12},{15,14},{17,16},{19,... | collective-permute-start | bytes 638984 | tf_op jit(solution)/shard_map/ppermute | solution.py:32
  22.1 6.0 %collective-permute-start.7 = (f32[26,4,1,512]{3,0,2,1:T(8,128)}, f32[26,4,1,512]{3,0,2,1:T(8,128)}, u32[]{:S(2)}, u32[]{:S(2)}) collective-permute-start(f32[26,4,1,512]{3,0,2,1:T(8,128)} %get-tuple-element.8), channel_id=1, source_target_pairs={{0,1},{2,3},{4,5},{6,7},{8,9},{10,11},{12,13},{14,15},{16,17},{18,... | collective-permute-start | bytes 638984 | tf_op jit(solution)/shard_map/ppermute | solution.py:31
  28.1 1.2 %fusion.20 = (f32[26,4,8,1]{3,0,2,1:T(8,128)}, f32[26,4,8,1]{3,0,2,1:T(8,128)}) fusion(f32[26,4,8,512]{3,0,2,1:T(8,128)S(1)} %copy.66), kind=kLoop, calls=%fused_computation.49 | loop fusion | bytes 13312 | tf_op jit(solution)/shard_map/slice | solution.py:29
  29.3 2.0 %collective-permute-start.4 = (f32[26,4,8,1]{3,0,2,1:T(8,128)}, f32[26,4,8,1]{3,0,2,1:T(8,128)}, u32[]{:S(2)}, u32[]{:S(2)}) collective-permute-start(f32[26,4,8,1]{3,0,2,1:T(8,128)} %get-tuple-element.5), channel_id=1, source_target_pairs={{0,2},{2,4},{4,6},{6,0},{1,3},{3,5},{5,7},{7,1},{8,10},{10,12},{12... | collective-permute-start | bytes 9992 | tf_op jit(solution)/shard_map/ppermute | solution.py:31
  32.0 8.3 %all-to-all-done = f32[1,208,512]{1,0,2:T(1,128)S(1)} async-done(((f32[1,208,512]{1,0,2:T(1,128)}), f32[1,208,512]{1,0,2:T(1,128)S(1)}, u32[]{:S(2)}, u32[]{:S(2)}) %all-to-all-start) | async-done | bytes 426016 | tf_op jit(solution)/shard_map/all_to_all | solution.py:48
  40.3 0.3 copy.58
  40.7 0.8 pad_maximum_fusion.5
  41.5 3.5 %all-to-all-start.1 = ((f32[4,1,208,128]{3,2,1,0:T(8,128)}), f32[4,1,208,128]{3,2,1,0:T(8,128)S(1)}, u32[]{:S(2)}, u32[]{:S(2)}) async-start(f32[4,1,208,128]{3,2,1,0:T(8,128)} %pad_maximum_fusion.5), calls=%async_computation.1 | async-start | bytes 851968 | tf_op jit(solution)/shard_map/all_to_all | solution.py:14
  45.0 0.9 slice_bitcast_fusion.8
  45.9 1.0 %fusion.11 = f32[6,4,8,512]{3,0,2,1:T(8,128)} fusion(f32[26,4,8,512]{3,0,2,1:T(8,128)S(1)} %copy.66, f32[4,8,512]{2,1,0:T(8,128)S(1)} %get-tuple-element.10, f32[6]{0:T(128)S(1)} %copy-done.9, f32[4,8,512]{2,1,0:T(8,128)S(1)} %get-tuple-element.9, f32[6]{0:T(128)S(1)} %copy-done.10), kind=kLoop, calls=%fused_computation.27 | loop fusion | flops 393216 | bytes 917552 | tf_op jit(solution)/shard_map/sub | solution.py:124
  46.9 2.5 %slice_bitcast_fusion.1 = f32[20,32,512]{2,1,0:T(8,128)} fusion(f32[26,4,8,512]{3,2,1,0:T(8,128)} %param.11), kind=kLoop, calls=%fused_computation.18 | loop fusion | bytes 2621440
  49.4 9.3 %all-to-all-done.1 = f32[4,1,208,128]{3,2,1,0:T(8,128)S(1)} async-done(((f32[4,1,208,128]{3,2,1,0:T(8,128)}), f32[4,1,208,128]{3,2,1,0:T(8,128)S(1)}, u32[]{:S(2)}, u32[]{:S(2)}) %all-to-all-start.1) | async-done | bytes 426016 | tf_op jit(solution)/shard_map/all_to_all | solution.py:14
  59.0 1.0 %copy-done.3 = f32[20,32,512]{2,1,0:T(8,128)S(1)} copy-done((f32[20,32,512]{2,1,0:T(8,128)S(1)}, f32[20,32,512]{2,1,0:T(8,128)}, u32[]{:S(2)}) %copy-start.3) | copy-done | bytes 1310744
  60.2 3.2 %fusion.9 = f32[20,4,8,512]{3,0,2,1:T(8,128)} fusion(f32[4,8,512,20]{2,1,0,3:T(8,128)S(1)} %slice_bitcast_fusion, f32[20,20]{1,0:T(8,128)S(1)} %copy-done.8), kind=kOutput, calls=%fused_computation.15 | convolution fusion | flops 78643200 | bytes 2623040 | tf_op jit(solution)/shard_map/dot_general | solution.py:117
  63.4 10.1 %collective-permute-done.1 = f32[208,512]{1,0:T(8,128)S(1)} collective-permute-done((f32[208,512]{1,0:T(8,128)S(1)}, f32[208,512]{1,0:T(8,128)S(1)}, u32[]{:S(2)}, u32[]{:S(2)}) %collective-permute-start.1) | collective-permute-done | bytes 426016 | tf_op jit(solution)/shard_map/ppermute | solution.py:21
  73.9 3.8 %collective-permute-start.3 = (f32[208,128]{1,0:T(8,128)S(1)}, f32[208,128]{1,0:T(8,128)S(1)}, u32[]{:S(2)}, u32[]{:S(2)}) collective-permute-start(f32[208,128]{1,0:T(8,128)S(1)} %get-tuple-element.12), channel_id=1, source_target_pairs={{2,0},{4,2},{6,4},{0,6},{3,1},{5,3},{7,5},{1,7},{10,8},{12,10},{14... | collective-permute-start | bytes 319496 | tf_op jit(solution)/shard_map/ppermute | solution.py:32
  77.7 2.7 %collective-permute-done.2 = f32[208,128]{1,0:T(8,128)S(1)} collective-permute-done((f32[208,128]{1,0:T(8,128)S(1)}, f32[208,128]{1,0:T(8,128)S(1)}, u32[]{:S(2)}, u32[]{:S(2)}) %collective-permute-start.2) | collective-permute-done | bytes 106528 | tf_op jit(solution)/shard_map/ppermute | solution.py:31
  80.5 0.6 convolution_bitcast_fusion.1
  81.2 0.6 convolution_bitcast_fusion
  81.7 0.9 copy.61
  82.7 1.9 %reshape_reshape.3 = f32[26,8,512]{2,1,0:T(8,128)} reshape(f32[208,4,128]{2,1,0:T(4,128)} %copy.61) | data formatting | bytes 851968 | tf_op jit(solution)/shard_map/reshape;reshape | solution.py:105
  84.6 1.9 %fusion.12 = f32[26,1,8,512]{3,0,2,1:T(8,128)S(1)} fusion(f32[26,8,512]{2,1,0:T(8,128)} %param.18, f32[26,8,512]{2,0,1:T(8,128)} %copy-done.4, f32[26,8,512]{2,1,0:T(8,128)} %reshape_reshape.3, pred[]{:T(512)S(6)} %eq.12, pred[]{:T(512)S(6)} %eq.11), kind=kLoop, calls=%fused_computation.30 | loop fusion | flops 212992 | bytes 1703938 | tf_op jit(solution)/shard_map/broadcast_in_dim | solution.py:109
  86.5 3.3 %collective-permute-done.5 = f32[26,4,8,1]{3,0,2,1:T(8,128)} collective-permute-done((f32[26,4,8,1]{3,0,2,1:T(8,128)}, f32[26,4,8,1]{3,0,2,1:T(8,128)}, u32[]{:S(2)}, u32[]{:S(2)}) %collective-permute-start.5) | collective-permute-done | bytes 3360 | tf_op jit(solution)/shard_map/ppermute | solution.py:32
  89.9 6.2 %fusion.4 = f32[26,4,8,512]{3,0,2,1:T(8,128)S(1)} fusion(f32[26,4,8,512]{3,0,2,1:T(8,128)} %copy-done.1, f32[26,4,1,512]{3,0,2,1:T(8,128)} %collective-permute-done.7, f32[26,4,1,512]{3,0,2,1:T(8,128)} %collective-permute-done.6, f32[26,4,8,1]{3,0,2,1:T(8,128)} %collective-permute-done.5, f32[26,4,8,1]{3,0,2,1:T(8,128)} %collective-permute-done.4, ...), kind=kLoop, calls=%fused_computation.5 | loop fusion | flops 7667712 | bytes 7444992 | tf_op jit(solution)/shard_map/add | solution.py:128
  96.1 2.2 %copy.78 = f32[26,4,8,512]{3,2,1,0:T(8,128)} copy(f32[26,4,8,512]{3,0,2,1:T(8,128)S(1)} %fusion.4) | data formatting | bytes 3407872 | tf_op jit(solution)/shard_map/add | solution.py:128
  (43 shorter events, 1.4 us)
Async XLA Ops:
  0.0 81.1 %copy-start = (f32[4,128,128]{2,1,0:T(8,128)S(1)}, f32[4,128,128]{2,1,0:T(8,128)}, u32[]{:S(2)}) copy-start(f32[4,128,128]{2,1,0:T(8,128)} %param.19) | copy-start | bytes 786436
  2.5 75.2 %copy-start.1 = (f32[26,4,8,512]{3,0,2,1:T(8,128)}, f32[26,4,8,512]{3,0,2,1:T(8,128)S(1)}, u32[]{:S(2)}) copy-start(f32[26,4,8,512]{3,0,2,1:T(8,128)S(1)} %copy.66) | copy-start | bytes 5111812
  2.6 10.5 %collective-permute-start = (f32[26,8,512]{2,0,1:T(8,128)S(1)}, f32[26,8,512]{2,0,1:T(8,128)S(1)}, u32[]{:S(2)}, u32[]{:S(2)}) collective-permute-start(f32[26,8,512]{2,0,1:T(8,128)S(1)} %slice_bitcast_fusion.2), channel_id=1, source_target_pairs={{0,8},{8,16},{16,24},{1,9},{9,17},{17,25},{2,10},{10,18},{18,26},{... | collective-permute-start | bytes 1277960 | tf_op jit(solution)/shard_map/ppermute | solution.py:40
  13.1 0.8 copy-start.4
  15.1 25.1 %all-to-all-start = ((f32[1,208,512]{1,0,2:T(1,128)}), f32[1,208,512]{1,0,2:T(1,128)S(1)}, u32[]{:S(2)}, u32[]{:S(2)}) async-start(f32[1,208,512]{1,0,2:T(1,128)} %copy.57), calls=%async_computation | async-start | bytes 1048576 | tf_op jit(solution)/shard_map/all_to_all | solution.py:48
  20.9 69.0 %collective-permute-start.6 = (f32[26,4,1,512]{3,0,2,1:T(8,128)}, f32[26,4,1,512]{3,0,2,1:T(8,128)}, u32[]{:S(2)}, u32[]{:S(2)}) collective-permute-start(f32[26,4,1,512]{3,0,2,1:T(8,128)} %get-tuple-element.7), channel_id=1, source_target_pairs={{1,0},{3,2},{5,4},{7,6},{9,8},{11,10},{13,12},{15,14},{17,16},{19,... | collective-permute-start | bytes 638984 | tf_op jit(solution)/shard_map/ppermute | solution.py:32
  22.1 67.7 %collective-permute-start.7 = (f32[26,4,1,512]{3,0,2,1:T(8,128)}, f32[26,4,1,512]{3,0,2,1:T(8,128)}, u32[]{:S(2)}, u32[]{:S(2)}) collective-permute-start(f32[26,4,1,512]{3,0,2,1:T(8,128)} %get-tuple-element.8), channel_id=1, source_target_pairs={{0,1},{2,3},{4,5},{6,7},{8,9},{10,11},{12,13},{14,15},{16,17},{18,... | collective-permute-start | bytes 638984 | tf_op jit(solution)/shard_map/ppermute | solution.py:31
  29.3 57.2 %collective-permute-start.4 = (f32[26,4,8,1]{3,0,2,1:T(8,128)}, f32[26,4,8,1]{3,0,2,1:T(8,128)}, u32[]{:S(2)}, u32[]{:S(2)}) collective-permute-start(f32[26,4,8,1]{3,0,2,1:T(8,128)} %get-tuple-element.5), channel_id=1, source_target_pairs={{0,2},{2,4},{4,6},{6,0},{1,3},{3,5},{5,7},{7,1},{8,10},{10,12},{12... | collective-permute-start | bytes 9992 | tf_op jit(solution)/shard_map/ppermute | solution.py:31
  40.3 5.6 %copy-start.9 = (f32[6]{0:T(128)S(1)}, f32[6]{0:T(128)}, u32[]{:S(2)}) copy-start(f32[6]{0:T(128)} %param.17) | copy-start | bytes 76
  40.3 5.6 %copy-start.10 = (f32[6]{0:T(128)S(1)}, f32[6]{0:T(128)}, u32[]{:S(2)}) copy-start(f32[6]{0:T(128)} %param.16) | copy-start | bytes 76
  41.5 17.2 %all-to-all-start.1 = ((f32[4,1,208,128]{3,2,1,0:T(8,128)}), f32[4,1,208,128]{3,2,1,0:T(8,128)S(1)}, u32[]{:S(2)}, u32[]{:S(2)}) async-start(f32[4,1,208,128]{3,2,1,0:T(8,128)} %pad_maximum_fusion.5), calls=%async_computation.1 | async-start | bytes 851968 | tf_op jit(solution)/shard_map/all_to_all | solution.py:14
  58.7 1.3 %copy-start.3 = (f32[20,32,512]{2,1,0:T(8,128)S(1)}, f32[20,32,512]{2,1,0:T(8,128)}, u32[]{:S(2)}) copy-start(f32[20,32,512]{2,1,0:T(8,128)} %slice_bitcast_fusion.1) | copy-start | bytes 3932164
  58.7 1.5 %copy-start.8 = (f32[20,20]{1,0:T(8,128)S(1)}, f32[20,20]{1,0:T(8,128)}, u32[]{:S(2)}) copy-start(f32[20,20]{1,0:T(8,128)} %param.15) | copy-start | bytes 4804
  59.0 14.5 %collective-permute-start.1 = (f32[208,512]{1,0:T(8,128)S(1)}, f32[208,512]{1,0:T(8,128)S(1)}, u32[]{:S(2)}, u32[]{:S(2)}) collective-permute-start(f32[208,512]{1,0:T(8,128)S(1)} %bitcast.66), channel_id=1, source_target_pairs={{6,0},{0,2},{2,4},{4,6},{7,1},{1,3},{3,5},{5,7},{14,8},{8,10},{10,... | collective-permute-start | bytes 1277960 | tf_op jit(solution)/shard_map/ppermute | solution.py:21
  60.2 17.5 %copy-start.11 = (s32[4]{0:T(128)S(1)}, s32[4]{0:T(128)}, u32[]{:S(2)}) copy-start(s32[4]{0:T(128)} %param.20) | copy-start | bytes 52
  73.8 6.6 %collective-permute-start.2 = (f32[208,128]{1,0:T(8,128)S(1)}, f32[208,128]{1,0:T(8,128)S(1)}, u32[]{:S(2)}, u32[]{:S(2)}) collective-permute-start(f32[208,128]{1,0:T(8,128)S(1)} %get-tuple-element.11), channel_id=1, source_target_pairs={{0,2},{2,4},{4,6},{6,0},{1,3},{3,5},{5,7},{7,1},{8,10},{10,12},{12... | collective-permute-start | bytes 319496 | tf_op jit(solution)/shard_map/ppermute | solution.py:31
  73.9 6.5 %collective-permute-start.3 = (f32[208,128]{1,0:T(8,128)S(1)}, f32[208,128]{1,0:T(8,128)S(1)}, u32[]{:S(2)}, u32[]{:S(2)}) collective-permute-start(f32[208,128]{1,0:T(8,128)S(1)} %get-tuple-element.12), channel_id=1, source_target_pairs={{2,0},{4,2},{6,4},{0,6},{3,1},{5,3},{7,5},{1,7},{10,8},{12,10},{14... | collective-permute-start | bytes 319496 | tf_op jit(solution)/shard_map/ppermute | solution.py:32
  80.4 9.5 %collective-permute-start.5 = (f32[26,4,8,1]{3,0,2,1:T(8,128)}, f32[26,4,8,1]{3,0,2,1:T(8,128)}, u32[]{:S(2)}, u32[]{:S(2)}) collective-permute-start(f32[26,4,8,1]{3,0,2,1:T(8,128)} %get-tuple-element.6), channel_id=1, source_target_pairs={{2,0},{4,2},{6,4},{0,6},{3,1},{5,3},{7,5},{1,7},{10,8},{12,10},{14... | collective-permute-start | bytes 9992 | tf_op jit(solution)/shard_map/ppermute | solution.py:32
  81.1 8.8 %slice-start = ((f32[26,4,8,512]{3,0,2,1:T(8,128)}), f32[26,3,8,512]{3,0,2,1:T(8,128)S(1)}, s32[]{:S(2)}) async-start(f32[26,4,8,512]{3,0,2,1:T(8,128)} %copy-done.1), calls=%async_computation.2 | async-start | bytes 3145728 | tf_op jit(solution)/shard_map/slice | solution.py:109
  81.1 8.8 %copy-start.2 = (f32[20,4,8,512]{3,0,2,1:T(8,128)S(1)}, f32[20,4,8,512]{3,0,2,1:T(8,128)}, u32[]{:S(2)}) copy-start(f32[20,4,8,512]{3,0,2,1:T(8,128)} %fusion.9) | copy-start | bytes 3932164
  81.1 8.8 %copy-start.6 = (f32[4,8,512]{2,1,0:T(8,128)S(1)}, f32[4,8,512]{2,1,0:T(8,128)}, u32[]{:S(2)}) copy-start(f32[4,8,512]{2,1,0:T(8,128)} %param.14) | copy-start | bytes 196612
  81.1 8.8 %copy-start.7 = (f32[4,8,512]{2,1,0:T(8,128)S(1)}, f32[4,8,512]{2,1,0:T(8,128)}, u32[]{:S(2)}) copy-start(f32[4,8,512]{2,1,0:T(8,128)} %param.13) | copy-start | bytes 196612
  84.6 5.3 %copy-start.5 = (f32[6,4,8,512]{3,0,2,1:T(8,128)S(1)}, f32[6,4,8,512]{3,0,2,1:T(8,128)}, u32[]{:S(2)}) copy-start(f32[6,4,8,512]{3,0,2,1:T(8,128)} %fusion.11) | copy-start | bytes 1179652
